TPU v7x, 32 devices: a whole 2x2x4 slice. The times are simulated.
32 devices in a mesh: reg: 4 (over y, core), prod: 8 (over z, x).
Axes of the slice: x: 2, y: 2, z: 4, core: 2. Of those that a mesh axis runs over, the one named last changes fastest.
Arguments:
- bottom_series_predictions: float32 [128, 256, 128], P('reg', 'prod'), may hold values from -6 to 6
- group_item_predictions: float32 [32, 256, 128], P('reg', 'prod'), may hold values from -18 to 18
- area_class_predictions: float32 [128, 32, 128], P('reg', 'prod'), may hold values from -18 to 18
- group_class_predictions: float32 [32, 32, 128], P('reg'), may hold values from -48 to 48
- bottom_series_precision: float32 [128, 256], P('reg', 'prod'), may hold values from 0.5 to 5
- group_item_precision: float32 [32, 256], P('reg', 'prod'), may hold values from 0.02 to 0.5
- area_class_precision: float32 [128, 32], P('reg', 'prod'), may hold values from 0.02 to 0.5
- group_class_precision: float32 [32, 32], P('reg'), may hold values from 0.002 to 0.05
- group_area_partition: int32 [32, 128], replicated, may hold values from -1 to 127, as said below
- class_item_partition: int32 [32, 128], replicated, may hold values from -1 to 255, as said below
Outputs:
- solution_field: float32 [128, 256, 128], P('reg', 'prod')
- residual: float32 [128, 256, 128], P('reg', 'prod')
Inputs may be any that keep to these rules, and one draw needn't show every extreme that they name: `group_area_partition`: every region stands in exactly one row; each row holds its parent's regions in its first slots and -1 in the rest; a parent has 1 to 97 regions, and some parent has exactly 97. `class_item_partition`: every product stands in exactly one row; each row holds its category's products in its first slots and -1 in the rest; a category has 1 to 128 products, and some category has exactly 128.
All inputs are finite; a program needn't handle non-finite values.
Results may differ from a plain program's by a relative error of at most 0.00011.
Values sent between devices are 32-bit elements; how exact they have to be, the bound alone decides.
A program may use at most 64 MiB of HBM per device.

v0:
```python
import jax
import jax.numpy as jnp
from jax import lax
from jax.sharding import PartitionSpec as P

ITERATIONS = 2


def member_local(table, first, count):
    items = first + jnp.arange(count, dtype=jnp.int32)
    return jnp.any(table[:, :, None] == items[None, None, :], axis=1).astype(jnp.float32)


def on_device(
    bottom_series_predictions,
    group_item_predictions,
    area_class_predictions,
    group_class_predictions,
    bottom_series_precision,
    group_item_precision,
    area_class_precision,
    group_class_precision,
    group_area_partition,
    class_item_partition,
):
    high = lax.Precision.HIGHEST
    areas_overall, items_overall, horizon_length = bottom_series_predictions.shape
    area_index_table = member_local(
        group_area_partition, lax.axis_index("reg") * areas_overall, areas_overall
    )
    item_index_table = member_local(
        class_item_partition, lax.axis_index("prod") * items_overall, items_overall
    )
    parent_share = area_index_table.shape[0] // lax.axis_size("reg")

    def disaggregate_onto(upper, lower):
        block = area_index_table
        total = jnp.einsum(
            "pr,pqh->rqh", block, lax.all_gather(upper, "reg", axis=0, tiled=True), precision=high
        )
        block = item_index_table
        return total + jnp.einsum(
            "crh,cq->rqh", lax.all_gather(lower, "prod", axis=0, tiled=True), block, precision=high
        )

    def replicate_across(corner):
        return jnp.einsum("pch,cq->pqh", corner, item_index_table, precision=high)

    def operate(field):
        rows_local = jnp.einsum("pr,rqh->pqh", area_index_table, field, precision=high)
        row_share = lax.psum_scatter(rows_local, "reg", scatter_dimension=0, tiled=True)
        col_share = lax.psum_scatter(
            jnp.einsum("cq,rqh->crh", item_index_table, field, precision=high),
            "prod",
            scatter_dimension=0,
            tiled=True,
        )
        partial_corner = jnp.einsum("pqh,cq->pch", rows_local, item_index_table, precision=high)
        whole = lax.psum(partial_corner, ("reg", "prod"))
        corner_share = lax.dynamic_slice_in_dim(
            whole, lax.axis_index("reg") * parent_share, parent_share, 0
        )
        upper = group_item_precision[:, :, None] * row_share + replicate_across(
            group_class_precision[:, :, None] * corner_share
        )
        lower = jnp.transpose(area_class_precision)[:, :, None] * col_share
        return bottom_series_precision[:, :, None] * field + disaggregate_onto(upper, lower)

    major_axis_first = group_item_precision[:, :, None] * group_item_predictions + replicate_across(
        group_class_precision[:, :, None] * group_class_predictions
    )
    lower_leading = jnp.transpose(
        area_class_precision[:, :, None] * area_class_predictions, (1, 0, 2)
    )
    system_source_term = bottom_series_precision[
        :, :, None
    ] * bottom_series_predictions + disaggregate_onto(major_axis_first, lower_leading)

    def two_products(vector, image):
        return lax.psum((jnp.sum(vector * vector), jnp.sum(vector * image)), ("reg", "prod"))

    solution_field = jnp.zeros_like(system_source_term)
    residual = system_source_term
    image = operate(residual)
    norm_now, product = two_products(residual, image)
    alpha = norm_now / product
    direction, along = (residual, image)
    for step in range(ITERATIONS):
        solution_field = solution_field + alpha * direction
        residual = residual - alpha * along
        if step + 1 < ITERATIONS:
            image = operate(residual)
            norm_next, product = two_products(residual, image)
            ratio = norm_next / norm_now
            alpha = norm_next / (product - ratio * norm_next / alpha)
            direction = residual + ratio * direction
            along = image + ratio * along
            norm_now = norm_next
    return (solution_field, residual)


def solution(mesh):
    return jax.shard_map(
        on_device,
        mesh=mesh,
        in_specs=(
            P("reg", "prod", None),
            P("reg", "prod", None),
            P("reg", "prod", None),
            P("reg", None, None),
            P("reg", "prod"),
            P("reg", "prod"),
            P("reg", "prod"),
            P("reg", None),
            P(),
            P(),
        ),
        out_specs=(P("reg", "prod", None), P("reg", "prod", None)),
        check_vma=False,
    )
```

profile of v0, /device:TPU:12, one launch (start us, length us, event | category | flops | bytes accessed | tf_op | source)
XLA Modules:
  0.0 496.7 jit_solution(14481580540045878076)
XLA Ops:
  10.1 1.3 fusion.5
  11.4 6.9 %all_gather.18 = f32[32,32,128]{2,1,0:T(8,128)S(1)} all-gather(f32[8,32,128]{2,1,0:T(8,128)S(1)} %fusion.5), channel_id=1, replica_groups=mesh['reg'=4,'prod'=8] {'reg'}, dimensions={0}, use_global_device_ids=true | all-gather | bytes 655360 | tf_op jit(solution)/shard_map/all_gather | solution.py:39
  18.4 29.1 %all_gather.19 = f32[32,32,128]{2,1,0:T(8,128)S(1)} all-gather(f32[4,32,128]{2,1,0:T(8,128)S(1)} %fusion.24), channel_id=1, replica_groups=mesh['reg'=4,'prod'=8] {'prod'}, dimensions={0}, use_global_device_ids=true | all-gather | bytes 589824 | tf_op jit(solution)/shard_map/all_gather | solution.py:43
  48.9 1.3 fusion.2
  50.6 1.5 convolution_bitcast_fusion.1
  52.1 1.1 copy.80
  54.1 1.1 copy.86
  55.2 129.7 %all-reduce.5.cloned.1.call-done = f32[32,32,128]{2,1,0:T(8,128)} async-done(((f32[32,32,128]{2,1,0:T(8,128)}), f32[32,32,128]{2,1,0:T(8,128)}) %all-reduce.5.cloned.1.call-update) | async-done | bytes 524304 | tf_op jit(solution)/shard_map/psum | solution.py:59
  184.9 1.3 fusion.4
  186.2 6.5 %all_gather.20 = f32[32,32,128]{2,1,0:T(8,128)S(1)} all-gather(f32[8,32,128]{2,1,0:T(8,128)S(1)} %fusion.4), channel_id=1, replica_groups=mesh['reg'=4,'prod'=8] {'reg'}, dimensions={0}, use_global_device_ids=true | all-gather | bytes 655360 | tf_op jit(solution)/shard_map/all_gather | solution.py:39
  193.6 28.7 %all_gather.21 = f32[32,32,128]{2,1,0:T(8,128)S(1)} all-gather(f32[4,32,128]{2,1,0:T(8,128)S(1)} %broadcast_multiply_fusion.1), channel_id=1, replica_groups=mesh['reg'=4,'prod'=8] {'prod'}, dimensions={0}, use_global_device_ids=true | all-gather | bytes 589824 | tf_op jit(solution)/shard_map/all_gather | solution.py:43
  223.1 1.6 multiply_reduce_fusion.2
  224.7 43.1 %all-reduce.1 = (f32[]{:T(128)}, f32[]{:T(128)}) all-reduce(f32[]{:T(128)} %get-tuple-element.13, f32[]{:T(128)} %get-tuple-element.12), channel_id=1, replica_groups=mesh['reg'=4,'prod'=8] {'reg','prod'}, use_global_device_ids=true, to_apply=%region_3.0 | all-reduce | flops 2 | bytes 16 | tf_op jit(solution)/shard_map/psum | solution.py:80
  269.5 1.5 convolution_bitcast_fusion
  271.1 1.1 copy.90
  273.2 1.1 copy.96
  274.3 125.1 %all-reduce.7.cloned.1.call-done = f32[32,32,128]{2,1,0:T(8,128)} async-done(((f32[32,32,128]{2,1,0:T(8,128)}), f32[32,32,128]{2,1,0:T(8,128)}) %all-reduce.7.cloned.1.call-update) | async-done | bytes 524304 | tf_op jit(solution)/shard_map/psum | solution.py:59
  399.4 1.3 fusion.3
  400.7 6.5 %all_gather.22 = f32[32,32,128]{2,1,0:T(8,128)S(1)} all-gather(f32[8,32,128]{2,1,0:T(8,128)S(1)} %fusion.3), channel_id=1, replica_groups=mesh['reg'=4,'prod'=8] {'reg'}, dimensions={0}, use_global_device_ids=true | all-gather | bytes 655360 | tf_op jit(solution)/shard_map/all_gather | solution.py:39
  408.1 28.8 %all_gather.23 = f32[32,32,128]{2,1,0:T(8,128)S(1)} all-gather(f32[4,32,128]{2,1,0:T(8,128)S(1)} %broadcast_multiply_fusion), channel_id=1, replica_groups=mesh['reg'=4,'prod'=8] {'prod'}, dimensions={0}, use_global_device_ids=true | all-gather | bytes 589824 | tf_op jit(solution)/shard_map/all_gather | solution.py:43
  437.6 1.6 multiply_reduce_fusion
  439.2 42.9 %all-reduce = (f32[]{:T(128)}, f32[]{:T(128)}) all-reduce(f32[]{:T(128)} %get-tuple-element.11, f32[]{:T(128)} %get-tuple-element.10), channel_id=1, replica_groups=mesh['reg'=4,'prod'=8] {'reg','prod'}, use_global_device_ids=true, to_apply=%region_10.0 | all-reduce | flops 2 | bytes 16 | tf_op jit(solution)/shard_map/psum | solution.py:80
  486.9 1.1 copy.101
  488.0 1.1 copy.100
  (49 shorter events, 9.9 us)
Async XLA Ops:
  8.0 0.7 copy-start.5
  8.0 176.9 %all-reduce.5.cloned.1.call-start = ((), (), s32[]{:S(2)}) async-start(), calls=%async_computation.5 | async-start | bytes 1048576 | tf_op jit(solution)/shard_map/psum | solution.py:59
  8.7 0.7 copy-start.6
  9.4 0.7 copy-start.2
  9.4 0.7 copy-start.3
  11.4 6.9 %copy-start.1 = (f32[32,4,128]{2,1,0:T(4,128)S(1)}, f32[32,4,128]{2,1,0:T(4,128)}, u32[]{:S(2)}) copy-start(f32[32,4,128]{2,1,0:T(4,128)} %param.12) | copy-start | bytes 196612
  11.4 6.9 %copy-start.4 = (f32[32,4]{0,1:T(4,128)S(1)}, f32[32,4]{0,1:T(4,128)}, u32[]{:S(2)}) copy-start(f32[32,4]{0,1:T(4,128)} %param.16) | copy-start | bytes 1540
  47.5 0.7 copy-start.7
  47.5 1.4 copy-start
  52.1 132.8 %reduce-scatter.5.cloned.1.call-start = ((), (), s32[]{:S(2)}) async-start(), calls=%async_computation.4 | async-start | bytes 655360 | tf_op jit(solution)/shard_map/reduce_scatter | solution.py:51
  53.3 139.4 %reduce-scatter.7.cloned.1.call-start = ((), (), s32[]{:S(2)}) async-start(), calls=%async_computation.6 | async-start | bytes 589824 | tf_op jit(solution)/shard_map/reduce_scatter | solution.py:52
  55.2 344.2 %all-reduce.7.cloned.1.call-start = ((), (), s32[]{:S(2)}) async-start(), calls=%async_computation.8 | async-start | bytes 1048576 | tf_op jit(solution)/shard_map/psum | solution.py:59
  271.0 128.4 %reduce-scatter.9.cloned.1.call-start = ((), (), s32[]{:S(2)}) async-start(), calls=%async_computation.7 | async-start | bytes 655360 | tf_op jit(solution)/shard_map/reduce_scatter | solution.py:51
  272.2 134.9 %reduce-scatter.11.cloned.1.call-start = ((), (), s32[]{:S(2)}) async-start(), calls=%async_computation.9 | async-start | bytes 589824 | tf_op jit(solution)/shard_map/reduce_scatter | solution.py:52
Sparse Core Ops, SparseCore 0:
  52.2 132.6 all-reduce.4
  271.2 128.1 all-reduce.6
Sparse Core Ops, SparseCore 1:
  55.1 24.1 reduce-scatter.4
  83.0 63.4 reduce-scatter.6
  274.0 19.7 reduce-scatter.8
  297.7 63.5 reduce-scatter.10
where the time goes:
time: 498 us; the launch traced here: 497 us
  waiting for transfers between devices  255 us (51%)
  blocking collectives  192 us (39%)
  between operations  21.7 us (4%)
  matrix products  15.5 us (3%)
  local copies, waits for them, and re-layouts  8.02 us (2%)
    psum x2, waiting for transfers between devices, operate(): whole = lax.psum(partial_corner, ('reg', 'prod'))  255 us
    all_gather x3, blocking collectives, disaggregate_onto(): lax.all_gather(lower, 'prod', axis=0, tiled=True)  86.6 us
    psum x2, blocking collectives, two_products(): lax.psum((jnp.sum(vector * vector), jnp.sum(vector * image)), ('reg', 'pr...  86 us
    all_gather x3, blocking collectives, disaggregate_onto(): lax.all_gather(upper, 'reg', axis=0, tiled=True)  19.9 us
  transfers between devices with their start and end apart: 6, of which 2 were waited for; matrix products, arithmetic and copies ran while one was open for 2% of the time, Pallas kernels for 0%

commit v1 on v0

--- a/solution.py
+++ b/solution.py
@@ -4,6 +4,18 @@
 from jax.sharding import PartitionSpec as P
 
 ITERATIONS = 2
+
+
+def summed_around(x, axis, dim, contribution):
+    size, place, rows = (lax.axis_size(axis), lax.axis_index(axis), x.shape[dim])
+    ahead = [(i, (i + 1) % size) for i in range(size)]
+    held, total = (x, None)
+    for step in range(size):
+        upcoming = lax.ppermute(held, axis, ahead) if step < size - 1 else None
+        absorb = contribution(held, (place - step) % size * rows)
+        total = absorb if total is None else total + absorb
+        held = upcoming
+    return total
 
 
 def member_local(table, first, count):
@@ -39,8 +51,16 @@
             "pr,pqh->rqh", block, lax.all_gather(upper, "reg", axis=0, tiled=True), precision=high
         )
         block = item_index_table
-        return total + jnp.einsum(
-            "crh,cq->rqh", lax.all_gather(lower, "prod", axis=0, tiled=True), block, precision=high
+        return total + summed_around(
+            lower,
+            "prod",
+            0,
+            lambda shard, start: jnp.einsum(
+                "crh,cq->rqh",
+                shard,
+                lax.dynamic_slice_in_dim(block, start, shard.shape[0], axis=0),
+                precision=high,
+            ),
         )
 
     def replicate_across(corner):

time: 498 us -> 541 us (1.086)
  waiting for transfers between devices: 255 us -> 350 us
  blocking collectives: 192 us -> 115 us
  matrix products: 15.5 us -> 30.1 us
  starting transfers between devices: 0.44 us -> 10.5 us
    reduce_scatter x2, waiting for transfers between devices: 0.01 us -> 122 us  [operate(): lax.psum_scatter(jnp.einsum('cq,rqh->crh', item_index_table, field, preci...]
    psum x2, waiting for transfers between devices: 255 us -> 138 us  [operate(): whole = lax.psum(partial_corner, ('reg', 'prod'))]
    ppermute x0 -> x21, waiting for transfers between devices: none -> 89.8 us  [summed_around(): upcoming = lax.ppermute(held, axis, ahead) if step < size - 1 else None]
    all_gather x3 -> x0, blocking collectives: 86.6 us -> none  [disaggregate_onto(): lax.all_gather(lower, 'prod', axis=0, tiled=True)]
    ppermute x0 -> x21, starting transfers between devices: none -> 10.2 us  [summed_around(): upcoming = lax.ppermute(held, axis, ahead) if step < size - 1 else None]
    psum x2, blocking collectives: 86 us -> 95.1 us  [two_products(): lax.psum((jnp.sum(vector * vector), jnp.sum(vector * image)), ('reg', 'pr...]
    dot_general x3 -> x24, matrix products: 2.14 us -> 10.6 us  [disaggregate_onto(): jnp.einsum('crh,cq->rqh', shard, lax.dynamic_slice_in_dim(block, start, s...]
    dot_general x3, matrix products: 4.43 us -> 11.5 us  [disaggregate_onto(): jnp.einsum('pr,pqh->rqh', block, lax.all_gather(upper, 'reg', axis=0, til...]
  transfers between devices with their start and end apart: 6 -> 27, of which waited for: 2 -> 22; matrix products, arithmetic and copies ran while one was open for 2% -> 4% of each run, Pallas kernels for 0% -> 0%
where the time goes in v1:
time: 541 us; the launch traced here: 540 us
  waiting for transfers between devices  350 us (65%)
  blocking collectives  115 us (21%)
  matrix products  30.1 us (6%)
  between operations  21.7 us (4%)
  starting transfers between devices  10.5 us (2%)
  local copies, waits for them, and re-layouts  8.96 us (2%)
    psum x2, waiting for transfers between devices, operate(): whole = lax.psum(partial_corner, ('reg', 'prod'))  138 us
    reduce_scatter x2, waiting for transfers between devices, operate(): lax.psum_scatter(jnp.einsum('cq,rqh->crh', item_index_table, field, preci...  122 us
    psum x2, blocking collectives, two_products(): lax.psum((jnp.sum(vector * vector), jnp.sum(vector * image)), ('reg', 'pr...  95.1 us
    ppermute x21, waiting for transfers between devices, summed_around(): upcoming = lax.ppermute(held, axis, ahead) if step < size - 1 else None  89.8 us
    all_gather x3, blocking collectives, disaggregate_onto(): lax.all_gather(upper, 'reg', axis=0, tiled=True)  19.5 us
    dot_general x3, matrix products, disaggregate_onto(): jnp.einsum('pr,pqh->rqh', block, lax.all_gather(upper, 'reg', axis=0, til...  11.5 us
  transfers between devices with their start and end apart: 27, of which 22 were waited for; matrix products, arithmetic and copies ran while one was open for 4% of the time, Pallas kernels for 0%

profile of v1, /device:TPU:12, one launch (start us, length us, event | category | flops | bytes accessed | tf_op | source)
XLA Modules:
  0.0 540.3 jit_solution(8463734892457041524)
XLA Ops:
  13.1 6.5 %all_gather.9 = f32[32,32,128]{2,1,0:T(8,128)S(1)} all-gather(f32[8,32,128]{2,1,0:T(8,128)S(1)} %fusion.2), channel_id=1, replica_groups=mesh['reg'=4,'prod'=8] {'reg'}, dimensions={0}, use_global_device_ids=true | all-gather | bytes 655360 | tf_op jit(solution)/shard_map/all_gather | solution.py:51
  27.5 4.1 collective-permute-done.2
  32.0 4.7 collective-permute-done.3
  37.1 4.7 collective-permute-done.4
  42.4 6.0 %collective-permute-done.5 = f32[4,32,128]{2,0,1:T(4,128)S(1)} collective-permute-done((f32[4,32,128]{2,0,1:T(4,128)S(1)}, f32[4,32,128]{2,0,1:T(4,128)S(1)}, u32[]{:S(2)}, u32[]{:S(2)}) %collective-permute-start.5) | collective-permute-done | bytes 65568 | tf_op jit(solution)/shard_map/ppermute | solution.py:14
  48.9 6.5 %collective-permute-done.6 = f32[4,32,128]{2,0,1:T(4,128)S(1)} collective-permute-done((f32[4,32,128]{2,0,1:T(4,128)S(1)}, f32[4,32,128]{2,0,1:T(4,128)S(1)}, u32[]{:S(2)}, u32[]{:S(2)}) %collective-permute-start.6) | collective-permute-done | bytes 65568 | tf_op jit(solution)/shard_map/ppermute | solution.py:14
  65.4 63.5 %reduce-scatter.7.cloned.1.call-done = f32[4,32,128]{2,1,0:T(8,128)} async-done(((f32[32,32,128]{2,1,0:T(8,128)}), f32[4,32,128]{2,1,0:T(8,128)}) %reduce-scatter.7.cloned.1.call-update) | async-done | bytes 65552 | tf_op jit(solution)/shard_map/reduce_scatter | solution.py:72
  132.0 69.1 %all-reduce.5.cloned.1.call-done = f32[32,32,128]{2,1,0:T(8,128)} async-done(((f32[32,32,128]{2,1,0:T(8,128)}), f32[32,32,128]{2,1,0:T(8,128)}) %all-reduce.5.cloned.1.call-update) | async-done | bytes 524304 | tf_op jit(solution)/shard_map/psum | solution.py:79
  202.3 6.5 %all_gather.10 = f32[32,32,128]{2,1,0:T(8,128)S(1)} all-gather(f32[8,32,128]{2,1,0:T(8,128)S(1)} %fusion.1), channel_id=1, replica_groups=mesh['reg'=4,'prod'=8] {'reg'}, dimensions={0}, use_global_device_ids=true | all-gather | bytes 655360 | tf_op jit(solution)/shard_map/all_gather | solution.py:51
  214.8 4.4 collective-permute-done.9
  219.7 4.7 collective-permute-done.10
  224.9 4.7 collective-permute-done.11
  230.0 6.3 %collective-permute-done.12 = f32[4,32,128]{2,0,1:T(4,128)S(1)} collective-permute-done((f32[4,32,128]{2,0,1:T(4,128)S(1)}, f32[4,32,128]{2,0,1:T(4,128)S(1)}, u32[]{:S(2)}, u32[]{:S(2)}) %collective-permute-start.12) | collective-permute-done | bytes 65568 | tf_op jit(solution)/shard_map/ppermute | solution.py:14
  236.8 6.5 %collective-permute-done.13 = f32[4,32,128]{2,0,1:T(4,128)S(1)} collective-permute-done((f32[4,32,128]{2,0,1:T(4,128)S(1)}, f32[4,32,128]{2,0,1:T(4,128)S(1)}, u32[]{:S(2)}, u32[]{:S(2)}) %collective-permute-start.13) | collective-permute-done | bytes 65568 | tf_op jit(solution)/shard_map/ppermute | solution.py:14
  247.7 47.6 %all-reduce.1 = (f32[]{:T(128)}, f32[]{:T(128)}) all-reduce(f32[]{:T(128)} %get-tuple-element.13, f32[]{:T(128)} %get-tuple-element.12), channel_id=1, replica_groups=mesh['reg'=4,'prod'=8] {'reg','prod'}, use_global_device_ids=true, to_apply=%region_3.4 | all-reduce | flops 2 | bytes 16 | tf_op jit(solution)/shard_map/psum | solution.py:100
  301.6 58.2 %reduce-scatter.11.cloned.1.call-done = f32[4,32,128]{2,1,0:T(8,128)} async-done(((f32[32,32,128]{2,1,0:T(8,128)}), f32[4,32,128]{2,1,0:T(8,128)}) %reduce-scatter.11.cloned.1.call-update) | async-done | bytes 65552 | tf_op jit(solution)/shard_map/reduce_scatter | solution.py:72
  362.7 69.3 %all-reduce.7.cloned.1.call-done = f32[32,32,128]{2,1,0:T(8,128)} async-done(((f32[32,32,128]{2,1,0:T(8,128)}), f32[32,32,128]{2,1,0:T(8,128)}) %all-reduce.7.cloned.1.call-update) | async-done | bytes 524304 | tf_op jit(solution)/shard_map/psum | solution.py:79
  433.2 6.5 %all_gather.11 = f32[32,32,128]{2,1,0:T(8,128)S(1)} all-gather(f32[8,32,128]{2,1,0:T(8,128)S(1)} %fusion), channel_id=1, replica_groups=mesh['reg'=4,'prod'=8] {'reg'}, dimensions={0}, use_global_device_ids=true | all-gather | bytes 655360 | tf_op jit(solution)/shard_map/all_gather | solution.py:51
  445.8 4.4 collective-permute-done.16
  450.6 4.7 collective-permute-done.17
  455.8 4.7 collective-permute-done.18
  460.9 6.3 %collective-permute-done.19 = f32[4,32,128]{2,0,1:T(4,128)S(1)} collective-permute-done((f32[4,32,128]{2,0,1:T(4,128)S(1)}, f32[4,32,128]{2,0,1:T(4,128)S(1)}, u32[]{:S(2)}, u32[]{:S(2)}) %collective-permute-start.19) | collective-permute-done | bytes 65568 | tf_op jit(solution)/shard_map/ppermute | solution.py:14
  467.7 6.5 %collective-permute-done.20 = f32[4,32,128]{2,0,1:T(4,128)S(1)} collective-permute-done((f32[4,32,128]{2,0,1:T(4,128)S(1)}, f32[4,32,128]{2,0,1:T(4,128)S(1)}, u32[]{:S(2)}, u32[]{:S(2)}) %collective-permute-start.20) | collective-permute-done | bytes 65568 | tf_op jit(solution)/shard_map/ppermute | solution.py:14
  478.6 47.5 %all-reduce = (f32[]{:T(128)}, f32[]{:T(128)}) all-reduce(f32[]{:T(128)} %get-tuple-element.11, f32[]{:T(128)} %get-tuple-element.10), channel_id=1, replica_groups=mesh['reg'=4,'prod'=8] {'reg','prod'}, use_global_device_ids=true, to_apply=%region_10.11 | all-reduce | flops 2 | bytes 16 | tf_op jit(solution)/shard_map/psum | solution.py:100
  (113 shorter events, 64.6 us)
Async XLA Ops:
  8.0 120.9 %reduce-scatter.7.cloned.1.call-start = ((), (), s32[]{:S(2)}) async-start(), calls=%async_computation.6 | async-start | bytes 589824 | tf_op jit(solution)/shard_map/reduce_scatter | solution.py:72
  9.7 11.3 %collective-permute-start = (f32[4,32,128]{2,0,1:T(4,128)S(1)}, f32[4,32,128]{2,0,1:T(4,128)S(1)}, u32[]{:S(2)}, u32[]{:S(2)}) collective-permute-start(f32[4,32,128]{2,0,1:T(4,128)S(1)} %multiply_bitcast_fusion), channel_id=1, source_target_pairs={{0,1},{1,2},{2,3},{3,4},{4,5},{5,6},{6,7},{7,0},{8,9},{9,10},{10,1... | collective-permute-start | bytes 196616 | tf_op jit(solution)/shard_map/ppermute | solution.py:14
  21.1 5.3 collective-permute-start.1
  26.4 5.2 collective-permute-start.2
  31.5 5.2 collective-permute-start.3
  41.9 6.6 %collective-permute-start.5 = (f32[4,32,128]{2,0,1:T(4,128)S(1)}, f32[4,32,128]{2,0,1:T(4,128)S(1)}, u32[]{:S(2)}, u32[]{:S(2)}) collective-permute-start(f32[4,32,128]{2,0,1:T(4,128)S(1)} %collective-permute-done.4), channel_id=1, source_target_pairs={{0,1},{1,2},{2,3},{3,4},{4,5},{5,6},{6,7},{7,0},{8,9},{9,10},{10,1... | collective-permute-start | bytes 196616 | tf_op jit(solution)/shard_map/ppermute | solution.py:14
  48.5 7.0 %collective-permute-start.6 = (f32[4,32,128]{2,0,1:T(4,128)S(1)}, f32[4,32,128]{2,0,1:T(4,128)S(1)}, u32[]{:S(2)}, u32[]{:S(2)}) collective-permute-start(f32[4,32,128]{2,0,1:T(4,128)S(1)} %collective-permute-done.5), channel_id=1, source_target_pairs={{0,1},{1,2},{2,3},{3,4},{4,5},{5,6},{6,7},{7,0},{8,9},{9,10},{10,1... | collective-permute-start | bytes 196616 | tf_op jit(solution)/shard_map/ppermute | solution.py:14
  61.5 139.6 %all-reduce.5.cloned.1.call-start = ((), (), s32[]{:S(2)}) async-start(), calls=%async_computation.5 | async-start | bytes 1048576 | tf_op jit(solution)/shard_map/psum | solution.py:79
  63.4 137.6 %reduce-scatter.5.cloned.1.call-start = ((), (), s32[]{:S(2)}) async-start(), calls=%async_computation.4 | async-start | bytes 655360 | tf_op jit(solution)/shard_map/reduce_scatter | solution.py:71
  64.6 295.2 %reduce-scatter.11.cloned.1.call-start = ((), (), s32[]{:S(2)}) async-start(), calls=%async_computation.9 | async-start | bytes 589824 | tf_op jit(solution)/shard_map/reduce_scatter | solution.py:72
  129.8 79.0 %collective-permute-start.7 = (f32[4,32,128]{2,0,1:T(4,128)S(1)}, f32[4,32,128]{2,0,1:T(4,128)S(1)}, u32[]{:S(2)}, u32[]{:S(2)}) collective-permute-start(f32[4,32,128]{2,0,1:T(4,128)S(1)} %copy_multiply_fusion.2), channel_id=1, source_target_pairs={{0,1},{1,2},{2,3},{3,4},{4,5},{5,6},{6,7},{7,0},{8,9},{9,10},{10,1... | collective-permute-start | bytes 196616 | tf_op jit(solution)/shard_map/ppermute | solution.py:14
  208.8 5.2 collective-permute-start.8
  214.1 5.2 collective-permute-start.9
  219.2 5.2 collective-permute-start.10
  224.4 5.2 collective-permute-start.11
  229.6 6.8 %collective-permute-start.12 = (f32[4,32,128]{2,0,1:T(4,128)S(1)}, f32[4,32,128]{2,0,1:T(4,128)S(1)}, u32[]{:S(2)}, u32[]{:S(2)}) collective-permute-start(f32[4,32,128]{2,0,1:T(4,128)S(1)} %collective-permute-done.11), channel_id=1, source_target_pairs={{0,1},{1,2},{2,3},{3,4},{4,5},{5,6},{6,7},{7,0},{8,9},{9,10},{10,1... | collective-permute-start | bytes 196616 | tf_op jit(solution)/shard_map/ppermute | solution.py:14
  236.3 7.0 %collective-permute-start.13 = (f32[4,32,128]{2,0,1:T(4,128)S(1)}, f32[4,32,128]{2,0,1:T(4,128)S(1)}, u32[]{:S(2)}, u32[]{:S(2)}) collective-permute-start(f32[4,32,128]{2,0,1:T(4,128)S(1)} %collective-permute-done.12), channel_id=1, source_target_pairs={{0,1},{1,2},{2,3},{3,4},{4,5},{5,6},{6,7},{7,0},{8,9},{9,10},{10,1... | collective-permute-start | bytes 196616 | tf_op jit(solution)/shard_map/ppermute | solution.py:14
  298.5 133.5 %all-reduce.7.cloned.1.call-start = ((), (), s32[]{:S(2)}) async-start(), calls=%async_computation.8 | async-start | bytes 1048576 | tf_op jit(solution)/shard_map/psum | solution.py:79
  300.5 131.5 %reduce-scatter.9.cloned.1.call-start = ((), (), s32[]{:S(2)}) async-start(), calls=%async_computation.7 | async-start | bytes 655360 | tf_op jit(solution)/shard_map/reduce_scatter | solution.py:71
  360.8 79.0 %collective-permute-start.14 = (f32[4,32,128]{2,0,1:T(4,128)S(1)}, f32[4,32,128]{2,0,1:T(4,128)S(1)}, u32[]{:S(2)}, u32[]{:S(2)}) collective-permute-start(f32[4,32,128]{2,0,1:T(4,128)S(1)} %copy_multiply_fusion.1), channel_id=1, source_target_pairs={{0,1},{1,2},{2,3},{3,4},{4,5},{5,6},{6,7},{7,0},{8,9},{9,10},{10,1... | collective-permute-start | bytes 196616 | tf_op jit(solution)/shard_map/ppermute | solution.py:14
  439.7 5.2 collective-permute-start.15
  445.0 5.2 collective-permute-start.16
  460.5 6.8 %collective-permute-start.19 = (f32[4,32,128]{2,0,1:T(4,128)S(1)}, f32[4,32,128]{2,0,1:T(4,128)S(1)}, u32[]{:S(2)}, u32[]{:S(2)}) collective-permute-start(f32[4,32,128]{2,0,1:T(4,128)S(1)} %collective-permute-done.18), channel_id=1, source_target_pairs={{0,1},{1,2},{2,3},{3,4},{4,5},{5,6},{6,7},{7,0},{8,9},{9,10},{10,1... | collective-permute-start | bytes 196616 | tf_op jit(solution)/shard_map/ppermute | solution.py:14
  467.3 7.0 %collective-permute-start.20 = (f32[4,32,128]{2,0,1:T(4,128)S(1)}, f32[4,32,128]{2,0,1:T(4,128)S(1)}, u32[]{:S(2)}, u32[]{:S(2)}) collective-permute-start(f32[4,32,128]{2,0,1:T(4,128)S(1)} %collective-permute-done.19), channel_id=1, source_target_pairs={{0,1},{1,2},{2,3},{3,4},{4,5},{5,6},{6,7},{7,0},{8,9},{9,10},{10,1... | collective-permute-start | bytes 196616 | tf_op jit(solution)/shard_map/ppermute | solution.py:14
  (12 other events, 37.9 us)
Sparse Core Ops, SparseCore 0:
  61.6 67.2 reduce-scatter.6
  131.4 19.8 reduce-scatter.4
  298.6 61.1 reduce-scatter.10
  362.2 19.8 reduce-scatter.8
Sparse Core Ops, SparseCore 1:
  67.8 133.2 all-reduce.4
  304.9 127.1 all-reduce.6
